TPU v7x, 32 devices: a whole 2x2x4 slice. The times are simulated.
32 devices in a mesh: groups: 2 (over y), dp: 4 (over x, core), tensor: 4 (over z).
Axes of the slice: x: 2, y: 2, z: 4, core: 2. Of those that a mesh axis runs over, the one named last changes fastest.
Arguments:
- query: bfloat16 [4096, 512], P(('groups', 'dp'), 'tensor'), parts along dimension 0, may hold values from -4.5 to 4.5
- keys: bfloat16 [4096, 512], P(('groups', 'dp'), 'tensor'), parts along dimension 0, may hold values from -4.5 to 4.5
- values: bfloat16 [4096, 512], P(('groups', 'dp'), 'tensor'), parts along dimension 0, may hold values from -6 to 6
- upstream: bfloat16 [4096, 8192], P(('groups', 'dp', 'tensor')), parts along dimension 0, may hold values from -6 to 6
- projection: bfloat16 [512, 8192], P('tensor', 'dp'), may hold values from -0.0625 to 0.0625
- lengths: int32 [8, 8], P(('groups', 'dp')), parts along dimension 0, may hold values from 1 to 256, 512 in all within a row
Outputs:
- grad_query: bfloat16 [4096, 512], P(('groups', 'dp'), 'tensor'), parts along dimension 0
- grad_keys: bfloat16 [4096, 512], P(('groups', 'dp'), 'tensor'), parts along dimension 0
- grad_values: bfloat16 [4096, 512], P(('groups', 'dp'), 'tensor'), parts along dimension 0
- grad_projection: float32 [1024, 8192], P(('groups', 'tensor'), 'dp'), parts along dimension 0
There are 2 independent parts, one for each index of `groups`. A program takes and returns all parts, laid end to end along the dimension named above; an argument that names none is the same for every part. Nothing has to cross between parts.
Inputs may be any that keep to these rules, and one draw needn't show every extreme that they name: Each row holds the lengths of the 8 documents of one sequence in order; they sum to 512 and the largest is exactly 256.
All inputs are finite; a program needn't handle non-finite values.
Results may differ from a plain program's by a relative error of at most 0.014.
Values may be sent and summed in bfloat16 or wider, within the bound.
A program may use at most 64 MiB of HBM per device.

v0:
```python
import jax
import jax.numpy as jnp
from jax import lax
from jax.sharding import PartitionSpec as P

HD = 128


def sequence_mask(length_row, row_count):
    segment_ends = jnp.cumsum(length_row)
    places = jnp.arange(row_count, dtype=jnp.int32)
    labels = jnp.sum((segment_ends[None, :] <= places[:, None]).astype(jnp.int32), axis=1)
    same = labels[:, None] == labels[None, :]
    return jnp.logical_and(same, places[None, :] <= places[:, None])


def shards(query, keys, values, upstream, projection, lengths):
    row_count, width = query.shape
    head_count = width // HD
    scaling = HD ** (-0.5)
    allowed = sequence_mask(lengths[0], row_count)
    query_heads = query.reshape(row_count, head_count, HD)
    key_heads = keys.reshape(row_count, head_count, HD)
    value_heads = values.reshape(row_count, head_count, HD)
    scores = (
        jnp.einsum("qhd,khd->hqk", query_heads, key_heads, preferred_element_type=jnp.float32)
        * scaling
    )
    scores = jnp.where(allowed[None], scores, -1e30)
    row_max = jnp.max(scores, axis=2, keepdims=True)
    exponent = jnp.exp(scores - row_max)
    probs = exponent / jnp.sum(exponent, axis=2, keepdims=True)
    probs_low = probs.astype(jnp.bfloat16)
    attended = jnp.einsum(
        "hqk,khd->qhd", probs_low, value_heads, preferred_element_type=jnp.float32
    )
    attended = attended.astype(jnp.bfloat16).reshape(row_count, width)
    full_projection = lax.all_gather(projection, "dp", axis=1, tiled=True)
    gathered = lax.all_gather(upstream, "tensor", axis=0, tiled=True)
    out_total = lax.dot_general(
        gathered, full_projection, (((1,), (1,)), ((), ())), preferred_element_type=jnp.float32
    )
    partial_grad = lax.dot_general(
        attended, gathered, (((0,), (0,)), ((), ())), preferred_element_type=jnp.float32
    )
    grad_projection = lax.psum_scatter(
        partial_grad.astype(jnp.bfloat16), "dp", scatter_dimension=1, tiled=True
    ).astype(jnp.float32)
    out_grad = out_total.astype(jnp.bfloat16)
    grad_heads = out_grad.reshape(row_count, head_count, HD)
    grad_values = jnp.einsum(
        "hqk,qhd->khd", probs_low, grad_heads, preferred_element_type=jnp.float32
    ).astype(jnp.bfloat16)
    grad_probs = jnp.einsum(
        "qhd,khd->hqk", grad_heads, value_heads, preferred_element_type=jnp.float32
    )
    delta = jnp.sum(probs * grad_probs, axis=2, keepdims=True)
    grad_scores = (probs * (grad_probs - delta) * scaling).astype(jnp.bfloat16)
    grad_query = jnp.einsum(
        "hqk,khd->qhd", grad_scores, key_heads, preferred_element_type=jnp.float32
    ).astype(jnp.bfloat16)
    grad_keys = jnp.einsum(
        "hqk,qhd->khd", grad_scores, query_heads, preferred_element_type=jnp.float32
    ).astype(jnp.bfloat16)
    return (
        grad_query.reshape(row_count, width),
        grad_keys.reshape(row_count, width),
        grad_values.reshape(row_count, width),
        grad_projection,
    )


def solution(mesh):
    in_specs = (
        P(("groups", "dp"), "tensor"),
        P(("groups", "dp"), "tensor"),
        P(("groups", "dp"), "tensor"),
        P(("groups", "dp", "tensor"), None),
        P("tensor", "dp"),
        P(("groups", "dp"), None),
    )
    out_specs = (
        P(("groups", "dp"), "tensor"),
        P(("groups", "dp"), "tensor"),
        P(("groups", "dp"), "tensor"),
        P(("groups", "tensor"), "dp"),
    )
    return jax.shard_map(shards, mesh=mesh, in_specs=in_specs, out_specs=out_specs, check_vma=False)
```

profile of v0, /device:TPU:1, one launch (start us, length us, event | category | flops | bytes accessed | tf_op | source)
XLA Modules:
  0.0 225.8 jit_solution(17024745603641305551)
XLA Ops:
  7.2 0.0 copy-start
  7.2 0.0 all-gather.3.cloned.1.call-start
  7.2 0.7 all-gather.3.cloned.1.call-update
  7.9 0.0 all-gather.5.cloned.1.call-start
  8.0 0.7 all-gather.5.cloned.1.call-update
  8.7 0.0 reduce-scatter.2.cloned.1.call-start
  8.7 0.8 reduce-window.8
  9.5 0.1 convert_reduce_fusion
  9.6 1.3 fusion.11
  10.9 0.2 fusion.4
  11.1 150.3 %all-gather.3.cloned.1.call-done = bf16[512,8192]{1,0:T(8,128)(2,1)} async-done(((bf16[128,8192]{1,0:T(8,128)(2,1)}), bf16[512,8192]{1,0:T(8,128)(2,1)}) %all-gather.3.cloned.1.call-update) | async-done | bytes 8388624 | tf_op jit(solution)/shard_map/all_gather | solution.py:39
  161.4 0.0 copy-done
  161.4 6.5 %convolution_convert_fusion = bf16[128,8192]{1,0:T(8,128)(2,1)} fusion(bf16[512,8192]{1,0:T(8,128)(2,1)} %all-gather.3.cloned.1.call-done, bf16[512,128]{1,0:T(8,128)(2,1)S(1)} %copy-done, f32[512,512]{0,1:T(8,128)S(1)} %get-tuple-element.13, f32[512]{0:T(512)S(1)} %fusion.4, f32[512]{0:T(512)S(1)} %get-tuple-element.12), kind=kOutput, calls=%fused_computation | convolution fusion | flops 1142751232 | bytes 11669504 | tf_op jit(solution)/shard_map/dot_general | solution.py:43
  167.9 0.0 reduce-scatter.2.cloned.1.call-update
  167.9 16.1 %all-gather.5.cloned.1.call-done = bf16[128,8192]{1,0:T(8,128)(2,1)} async-done(((bf16[128,2048]{1,0:T(8,128)(2,1)}), bf16[128,8192]{1,0:T(8,128)(2,1)}) %all-gather.5.cloned.1.call-update) | async-done | bytes 2097168 | tf_op jit(solution)/shard_map/all_gather | solution.py:38
  184.0 6.3 %convolution_convert_fusion.5 = bf16[512,128]{1,0:T(8,128)(2,1)S(1)} fusion(bf16[512,8192]{1,0:T(8,128)(2,1)} %all-gather.3.cloned.1.call-done, bf16[128,8192]{1,0:T(8,128)(2,1)} %all-gather.5.cloned.1.call-done), kind=kOutput, calls=%fused_computation.7 | convolution fusion | flops 1073807360 | bytes 10616832 | tf_op jit(solution)/shard_map/dot_general | solution.py:40
  190.3 0.3 fusion.1
  190.7 0.0 copy-start.1
  190.7 0.0 copy-start.2
  190.7 0.8 copy.11
  191.5 0.3 multiply_reduce_fusion
  191.8 0.3 multiply_convert_fusion
  192.1 0.0 copy-done.1
  192.1 0.9 convolution_convert_fusion.3
  193.0 0.0 copy-done.2
  193.0 1.0 convolution_convert_fusion.4
  194.0 23.2 %reduce-scatter.2.cloned.1.call-done = bf16[128,2048]{1,0:T(8,128)(2,1)} async-done(((bf16[128,8192]{1,0:T(8,128)(2,1)}), bf16[128,2048]{1,0:T(8,128)(2,1)}) %reduce-scatter.2.cloned.1.call-update) | async-done | bytes 524304 | tf_op jit(solution)/shard_map/reduce_scatter | solution.py:46
  217.2 2.1 convert_element_type.58
Async XLA Ops:
  7.2 154.3 %copy-start = (bf16[512,128]{1,0:T(8,128)(2,1)S(1)}, bf16[512,128]{1,0:T(8,128)(2,1)}, u32[]{:S(2)}) copy-start(bf16[512,128]{1,0:T(8,128)(2,1)} %param.8) | copy-start | bytes 393220
  7.2 154.3 %all-gather.3.cloned.1.call-start = ((), (), s32[]{:S(2)}) async-start(), calls=%async_computation.1 | async-start | bytes 10485760 | tf_op jit(solution)/shard_map/all_gather | solution.py:39
  7.9 176.1 %all-gather.5.cloned.1.call-start = ((), (), s32[]{:S(2)}) async-start(), calls=%async_computation.2 | async-start | bytes 2621440 | tf_op jit(solution)/shard_map/all_gather | solution.py:38
  8.7 208.5 %reduce-scatter.2.cloned.1.call-start = ((), (), s32[]{:S(2)}) async-start(), calls=%async_computation.3 | async-start | bytes 2621440 | tf_op jit(solution)/shard_map/reduce_scatter | solution.py:46
  190.7 1.4 copy-start.1
  190.7 2.3 %copy-start.2 = (bf16[512,128]{1,0:T(8,128)(2,1)S(1)}, bf16[512,128]{1,0:T(8,128)(2,1)}, u32[]{:S(2)}) copy-start(bf16[512,128]{1,0:T(8,128)(2,1)} %param.7) | copy-start | bytes 393220
Sparse Core Ops, SparseCore 0:
  9.6 151.8 all-gather.2
  163.0 20.9 all-gather.4
  186.5 30.6 reduce-scatter.1
where the time goes:
time: 227 us; the launch traced here: 226 us
  waiting for transfers between devices  191 us (84%)
  matrix products  16.7 us (7%)
  between operations  13.8 us (6%)
  other arithmetic  3.52 us (2%)
    all_gather x1, waiting for transfers between devices, shards(): gathered = lax.all_gather(upstream, 'tensor', axis=0, tiled=True)  150 us
    reduce_scatter x1, waiting for transfers between devices, shards(): lax.psum_scatter(partial_grad.astype(jnp.bfloat16), 'dp', scatter_dimensi...  23.2 us
    all_gather x1, waiting for transfers between devices, shards(): full_projection = lax.all_gather(projection, 'dp', axis=1, tiled=True)  16.1 us
    dot_general x1, matrix products, shards(): lax.dot_general(attended, gathered, (((0,), (0,)), ((), ())), preferred_e...  6.48 us
    dot_general x1, matrix products, shards(): lax.dot_general(gathered, full_projection, (((1,), (1,)), ((), ())), pref...  6.31 us
  transfers between devices with their start and end apart: 3, of which 3 were waited for; matrix products, arithmetic and copies ran while one was open for 8% of the time, Pallas kernels for 0%

commit v1 on v0

--- a/solution.py
+++ b/solution.py
@@ -1,9 +1,20 @@
+import functools
+
 import jax
 import jax.numpy as jnp
 from jax import lax
+from jax.experimental import pallas as pl
+from jax.experimental.pallas import tpu as pltpu
 from jax.sharding import PartitionSpec as P
 
 HD = 128
+MESH = pl.DeviceIdType.MESH
+LANES = 128
+CHUNKS = 4
+HALVES = 2
+MOST_STEPS = 8
+F32 = jnp.float32
+BF16 = jnp.bfloat16
 
 
 def sequence_mask(length_row, row_count):
@@ -14,7 +25,7 @@
     return jnp.logical_and(same, places[None, :] <= places[:, None])
 
 
-def shards(query, keys, values, upstream, projection, lengths):
+def plain_shards(query, keys, values, upstream, projection, lengths):
     row_count, width = query.shape
     head_count = width // HD
     scaling = HD ** (-0.5)
@@ -70,7 +81,335 @@
     )
 
 
+def dot(a, b, over_a, over_b):
+    return lax.dot_general(
+        a, b, (((over_a,), (over_b,)), ((), ())), preferred_element_type=F32
+    )
+
+
+def kernel(
+    seqs, line, chunks,
+    query, keys, values, upstream, projection, lengths,
+    grad_query, grad_keys, grad_values, grad_projection,
+    probs_ref, att_own, att_all, up_all, proj_all, part, part_in, og_own, og_in, stage, landed,
+    up_send, up_recv, right_send, left_send, proj_recv, att_send, att_recv, spread_send,
+    spread_recv, part_send, part_recv, og_send, og_recv, sum_send, sum_recv,
+):
+    d = lax.axis_index("dp")
+    t = lax.axis_index("tensor")
+    total = query.shape[0]
+    rows, _ = upstream.shape
+    high, features = projection.shape
+    wide = features // chunks
+    half = high // HALVES
+    scaling = HD ** (-0.5)
+    pending = []
+
+    def copy(src, dst, send_sem, recv_sem, to_d, to_t):
+        return pltpu.make_async_remote_copy(
+            src_ref=src, dst_ref=dst, send_sem=send_sem, recv_sem=recv_sem,
+            device_id={"dp": to_d, "tensor": to_t}, device_id_type=MESH,
+        )
+
+    barrier = pltpu.get_barrier_semaphore()
+    for k in range(1, seqs):
+        pl.semaphore_signal(
+            barrier, inc=1, device_id={"dp": lax.rem(d + k, seqs), "tensor": t},
+            device_id_type=MESH,
+        )
+    for k in range(1, line):
+        pl.semaphore_signal(
+            barrier, inc=1, device_id={"dp": d, "tensor": lax.rem(t + k, line)},
+            device_id_type=MESH,
+        )
+    pl.semaphore_wait(barrier, seqs + line - 2)
+
+    others = [lax.rem(d + k, seqs) for k in range(1, seqs)]
+    peers = [lax.rem(t + k, line) for k in range(1, line)]
+    mine = pl.ds(pl.multiple_of(d * rows, rows), rows)
+    right = jnp.minimum(t + 1, line - 1)
+    left = jnp.maximum(t - 1, 0)
+
+    def send_upstream(c):
+        for o in others:
+            off = pl.multiple_of(o * features + c * wide, wide)
+            one = copy(
+                upstream.at[:, pl.ds(off, wide)], up_all.at[c, mine],
+                up_send.at[o, c], up_recv.at[d, c], o, t,
+            )
+            one.start()
+            pending.append((None, one))
+
+    waited = set()
+
+    def wait_upstream(c):
+        if c in waited:
+            return
+        waited.add(c)
+        for o in others:
+            dst = up_all.at[c, pl.ds(pl.multiple_of(o * rows, rows), rows)]
+            copy(dst, dst, up_send.at[o, c], up_recv.at[o, c], o, t).wait_recv()
+
+    def block(j, p):
+        return proj_all.at[pl.ds(pl.multiple_of(j * high + p * half, half), half)]
+
+    def proj_send(j, p, source, where, toward):
+        sems = right_send if toward is right else left_send
+        one = copy(source, block(j, p), sems.at[j, p], proj_recv.at[j, p], d, toward)
+
+        @pl.when(where)
+        def _():
+            one.start()
+
+        pending.append((where, one))
+
+    def proj_own(p):
+        source = projection.at[pl.ds(p * half, half)]
+        proj_send(t, p, source, t < line - 1, right)
+        proj_send(t, p, source, t > 0, left)
+
+    def proj_step(k):
+        for p in range(HALVES):
+            from_left, from_right = jnp.maximum(t - k, 0), jnp.minimum(t + k, line - 1)
+            for j, here, toward, on in (
+                (from_left, t >= k, right, t < line - 1),
+                (from_right, t + k < line, left, t > 0),
+            ):
+                dst = block(j, p)
+
+                @pl.when(here)
+                def _(dst=dst, j=j):
+                    copy(dst, dst, right_send.at[j, p], proj_recv.at[j, p], d, right).wait_recv()
+
+                if k < line - 1:
+                    proj_send(j, p, dst, jnp.logical_and(here, on), toward)
+
+    early = max(1, chunks // 2)
+    for c in range(early):
+        send_upstream(c)
+    proj_own(0)
+
+    ends = []
+    sofar = lengths[0, 0]
+    for n in range(lengths.shape[1]):
+        ends.append(sofar)
+        if n + 1 < lengths.shape[1]:
+            sofar = sofar + lengths[0, n + 1]
+    down = lax.broadcasted_iota(jnp.int32, (total, 1), 0)
+    across = lax.broadcasted_iota(jnp.int32, (1, total), 1)
+    label_down = sum((down >= e).astype(jnp.int32) for e in ends)
+    label_across = sum((across >= e).astype(jnp.int32) for e in ends)
+    for q in range(line):
+        span = slice(q * rows, (q + 1) * rows)
+        scores = dot(query[span, :], keys[...], 1, 1) * scaling
+        allowed = jnp.logical_and(label_down[span] == label_across, across <= down[span])
+        scores = jnp.where(allowed, scores, -1e30)
+        exponent = jnp.exp(scores - jnp.max(scores, axis=1, keepdims=True))
+        probs = exponent / jnp.sum(exponent, axis=1, keepdims=True)
+        probs_ref[span, :] = probs
+        att_own[q] = dot(probs.astype(BF16), values[...], 1, 0).astype(BF16)
+    att_all[t, mine] = att_own[t]
+    for o in peers:
+        one = copy(
+            att_own.at[o], att_all.at[t, mine], att_send.at[o], att_recv.at[t], d, o
+        )
+        one.start()
+        pending.append((None, one))
+    for p in range(1, HALVES):
+        proj_own(p)
+    for c in range(chunks):
+        up_all[c, mine] = upstream[:, pl.ds(pl.multiple_of(d * features + c * wide, wide), wide)]
+    proj_all[pl.ds(pl.multiple_of(t * high, high), high), :] = projection[...]
+    for o in peers:
+        dst = att_all.at[o, mine]
+        copy(dst, dst, att_send.at[o], att_recv.at[o], d, o).wait_recv()
+    for o in others:
+        one = copy(
+            att_all.at[:, mine], att_all.at[:, mine], spread_send.at[o], spread_recv.at[d], o, t
+        )
+        one.start()
+        pending.append((None, one))
+    for c in range(early, chunks):
+        send_upstream(c)
+    proj_step(1)
+    for o in others:
+        dst = att_all.at[:, pl.ds(pl.multiple_of(o * rows, rows), rows)]
+        copy(dst, dst, spread_send.at[o], spread_recv.at[o], o, t).wait_recv()
+
+    def sum_chunk(c):
+        wait_upstream(c)
+        for k in range(line - 1, 0, -1):
+            for way, head, go, first, toward in (
+                (0, jnp.minimum(t + k, line - 1), t + k < line, t == 0, right),
+                (1, jnp.maximum(t - k, 0), t >= k, t == line - 1, left),
+            ):
+                one = copy(
+                    stage.at[way, head, c], landed.at[way, head, c],
+                    sum_send.at[way, head, c], sum_recv.at[way, head, c], d, toward,
+                )
+
+                @pl.when(go)
+                def _(way=way, head=head, first=first, one=one):
+                    term = dot(att_all[head], up_all[c], 0, 0)
+
+                    @pl.when(first)
+                    def _():
+                        stage[way, head, c] = term.astype(BF16)
+
+                    @pl.when(jnp.logical_not(first))
+                    def _():
+                        one.wait_recv()
+                        stage[way, head, c] = (
+                            term + landed[way, head, c].astype(F32)
+                        ).astype(BF16)
+
+                    one.start()
+
+                pending.append((go, one))
+
+    def own_chunk(c):
+        cols = slice(c * wide, (c + 1) * wide)
+        grad_projection[:, cols] = dot(att_all[t], up_all[c], 0, 0)
+        for way, there in ((0, t > 0), (1, t < line - 1)):
+            dst = landed.at[way, t, c]
+
+            @pl.when(there)
+            def _(way=way, dst=dst):
+                copy(
+                    dst, dst, sum_send.at[way, t, c], sum_recv.at[way, t, c], d, right
+                ).wait_recv()
+                grad_projection[:, cols] += landed[way, t, c].astype(F32)
+
+    def out_partials():
+        for c in range(chunks):
+            wait_upstream(c)
+        for o in others + [d]:
+            at = pl.ds(pl.multiple_of(o * rows, rows), rows)
+            piece = dot(up_all[0, at], proj_all[:, :wide], 1, 1)
+            for c in range(1, chunks):
+                piece += dot(up_all[c, at], proj_all[:, c * wide:(c + 1) * wide], 1, 1)
+            if o is d:
+                part_in[d] = piece.astype(BF16)
+                continue
+            part[o] = piece.astype(BF16)
+            one = copy(part.at[o], part_in.at[d], part_send.at[o], part_recv.at[d], o, t)
+            one.start()
+            pending.append((None, one))
+
+    def out_sum():
+        for o in others:
+            dst = part_in.at[o]
+            copy(dst, dst, part_send.at[o], part_recv.at[o], o, t).wait_recv()
+        whole = sum(part_in[n].astype(F32) for n in range(seqs)).astype(BF16)
+        for q in range(line):
+            og_own[q] = whole[:, q * HD:(q + 1) * HD]
+        og_in[t] = og_own[t]
+        for o in peers:
+            one = copy(og_own.at[o], og_in.at[t], og_send.at[o], og_recv.at[t], d, o)
+            one.start()
+            pending.append((None, one))
+
+    for c in range(chunks):
+        sum_chunk(c)
+        if c == 0:
+            for k in range(2, line):
+                proj_step(k)
+        if c == max(0, chunks - 3):
+            out_partials()
+        if c == max(0, chunks - 2):
+            out_sum()
+
+    for o in peers:
+        dst = og_in.at[o]
+        copy(dst, dst, og_send.at[o], og_recv.at[o], d, o).wait_recv()
+    grads = [og_in[q] for q in range(line)]
+    gv = 0.0
+    gk = 0.0
+    for q in range(line):
+        span = slice(q * rows, (q + 1) * rows)
+        probs = probs_ref[span, :]
+        gv = gv + dot(probs.astype(BF16), grads[q], 0, 0)
+        grad_probs = dot(grads[q], values[...], 1, 1)
+        delta = jnp.sum(probs * grad_probs, axis=1, keepdims=True)
+        grad_scores = (probs * (grad_probs - delta) * scaling).astype(BF16)
+        grad_query[span, :] = dot(grad_scores, keys[...], 1, 0).astype(BF16)
+        gk = gk + dot(grad_scores, query[span, :], 0, 0)
+    grad_values[...] = gv.astype(BF16)
+    grad_keys[...] = gk.astype(BF16)
+    for c in range(chunks):
+        own_chunk(c)
+
+    for where, one in pending:
+        if where is None:
+            one.wait_send()
+        else:
+
+            @pl.when(where)
+            def _(one=one):
+                one.wait_send()
+
+
+def fused_shards(seqs, line, query, keys, values, upstream, projection, lengths):
+    total, width = query.shape
+    rows = upstream.shape[0]
+    high, features = projection.shape
+    chunks = CHUNKS
+    wide = features // chunks
+    dma = pltpu.SemaphoreType.DMA
+    vmem = pltpu.VMEM
+    whole = pl.BlockSpec(memory_space=pltpu.VMEM)
+    return pl.pallas_call(
+        functools.partial(kernel, seqs, line, chunks),
+        out_shape=(
+            jax.ShapeDtypeStruct(query.shape, BF16),
+            jax.ShapeDtypeStruct(query.shape, BF16),
+            jax.ShapeDtypeStruct(query.shape, BF16),
+            jax.ShapeDtypeStruct(projection.shape, F32),
+        ),
+        in_specs=[whole] * 5 + [pl.BlockSpec(memory_space=pltpu.SMEM)],
+        out_specs=(whole,) * 4,
+        scratch_shapes=[
+            vmem((total, total), F32),
+            vmem((line, rows, width), BF16),
+            vmem((line, seqs * rows, width), BF16),
+            vmem((chunks, seqs * rows, wide), BF16),
+            vmem((line * high, features), BF16),
+            vmem((seqs, rows, line * high), BF16),
+            vmem((seqs, rows, line * high), BF16),
+            vmem((line, rows, width), BF16),
+            vmem((line, rows, width), BF16),
+            vmem((2, line, chunks, high, wide), BF16),
+            vmem((2, line, chunks, high, wide), BF16),
+            dma((seqs, chunks)), dma((seqs, chunks)),
+            dma((line, HALVES)), dma((line, HALVES)), dma((line, HALVES)),
+            dma((line,)), dma((line,)),
+            dma((seqs,)), dma((seqs,)),
+            dma((seqs,)), dma((seqs,)),
+            dma((line,)), dma((line,)),
+            dma((2, line, chunks)), dma((2, line, chunks)),
+        ],
+        compiler_params=pltpu.CompilerParams(collective_id=0, has_side_effects=True),
+    )(query, keys, values, upstream, projection, lengths)
+
+
 def solution(mesh):
+    seqs, line = mesh.shape["dp"], mesh.shape["tensor"]
+
+    def shards(query, keys, values, upstream, projection, lengths):
+        fits = (
+            query.shape[1] == HD
+            and projection.shape[0] == HD
+            and 1 < seqs
+            and 1 < line
+            and max(seqs, line) <= MOST_STEPS
+            and projection.shape[1] % (CHUNKS * LANES) == 0
+            and upstream.shape[0] % (2 * HALVES * 8) == 0
+            and upstream.shape[0] * line == query.shape[0]
+        )
+        if fits:
+            return fused_shards(seqs, line, query, keys, values, upstream, projection, lengths)
+        return plain_shards(query, keys, values, upstream, projection, lengths)
+
     in_specs = (
         P(("groups", "dp"), "tensor"),
         P(("groups", "dp"), "tensor"),

time: 227 us -> 95.1 us (0.42)
  waiting for transfers between devices: 191 us -> 0 us
  Pallas kernels: 0 us -> 85.6 us
  matrix products: 16.7 us -> 0 us
  between operations: 13.8 us -> 0.64 us
  local copies, waits for them, and re-layouts: 0.78 us -> 7 us
  other arithmetic: 3.52 us -> 0 us
    all_gather x2 -> x0, waiting for transfers between devices: 166 us -> none  [the longest x1 150 us: shards(): gathered = lax.all_gather(upstream, 'tensor', axis=0, tiled=True)]
    pallas_call x0 -> x1, Pallas kernels: none -> 85.6 us  [fused_shards(): pl.pallas_call(functools.partial(kernel, seqs, line, chunks), out_shape=(...]
    reduce_scatter x1 -> x0, waiting for transfers between devices: 23.2 us -> none  [shards(): lax.psum_scatter(partial_grad.astype(jnp.bfloat16), 'dp', scatter_dimensi...]
    dot_general x7 -> x0, matrix products: 16.7 us -> none  [the longest x1 6.48 us: shards(): lax.dot_general(attended, gathered, (((0,), (0,)), ((), ())), preferred_e...]
    unnamed x7 -> x4, local copies, waits for them, and re-layouts: 0.78 us -> 7 us
    convert_element_type x2 -> x0, other arithmetic: 2.41 us -> none  [the longest x1 2.12 us: shards(): grad_projection = lax.psum_scatter(partial_grad.astype(jnp.bfloat16), 'dp...]
  transfers between devices with their start and end apart: 3 -> 0, of which waited for: 3 -> 0; matrix products, arithmetic and copies ran while one was open for 8% -> 0% of each run, Pallas kernels for 0% -> 0%
where the time goes in v1:
time: 95.1 us; the launch traced here: 93.2 us
  Pallas kernels  85.6 us (90%)
  local copies, waits for them, and re-layouts  7 us (7%)
    pallas_call x1, Pallas kernels, fused_shards(): pl.pallas_call(functools.partial(kernel, seqs, line, chunks), out_shape=(...  85.6 us
    unnamed x4, local copies, waits for them, and re-layouts  7 us

profile of v1, /device:TPU:1, one launch (start us, length us, event | category | flops | bytes accessed | tf_op | source)
XLA Modules:
  0.0 93.2 jit_solution(11227356168788894501)
XLA Ops:
  0.6 85.6 %shard_map.93 = (bf16[512,128]{1,0:T(8,128)(2,1)}, bf16[512,128]{1,0:T(8,128)(2,1)}, bf16[512,128]{1,0:T(8,128)(2,1)}, f32[128,2048]{1,0:T(8,128)}) custom-call(bf16[512,128]{1,0:T(8,128)(2,1)} %query.1, bf16[512,128]{1,0:T(8,128)(2,1)} %keys.1, bf16[512,128]{1,0:T(8,128)(2,1)} %values.1, bf16[128,8192]{1,0:T(8,128)(2,1)} %upstream.1, ...), custom_call_target="tpu_custom_call" | custom-call | tf_op jit(solution)/shard_map/pallas_call | solution.py:361
  86.2 1.6 %copy.14 = bf16[512,128]{1,0:T(8,128)(2,1)} copy(bf16[512,128]{1,0:T(8,128)(2,1)} %get-tuple-element.8) | data formatting | bytes 262144
  87.8 1.6 %copy.15 = bf16[512,128]{1,0:T(8,128)(2,1)} copy(bf16[512,128]{1,0:T(8,128)(2,1)} %get-tuple-element.9) | data formatting | bytes 262144
  89.4 1.6 %copy.16 = bf16[512,128]{1,0:T(8,128)(2,1)} copy(bf16[512,128]{1,0:T(8,128)(2,1)} %get-tuple-element.10) | data formatting | bytes 262144
  90.9 2.3 %copy.17 = f32[128,2048]{1,0:T(8,128)} copy(f32[128,2048]{1,0:T(8,128)} %get-tuple-element.11) | data formatting | bytes 2097152

commit v2 on v1

--- a/solution.py
+++ b/solution.py
@@ -11,7 +11,6 @@
 MESH = pl.DeviceIdType.MESH
 LANES = 128
 CHUNKS = 4
-HALVES = 2
 MOST_STEPS = 8
 F32 = jnp.float32
 BF16 = jnp.bfloat16
@@ -92,7 +91,7 @@
     query, keys, values, upstream, projection, lengths,
     grad_query, grad_keys, grad_values, grad_projection,
     probs_ref, att_own, att_all, up_all, proj_all, part, part_in, og_own, og_in, stage, landed,
-    up_send, up_recv, right_send, left_send, proj_recv, att_send, att_recv, spread_send,
+    up_send, up_recv, right_send, left_send, proj_recv, swap_send, swap_recv, att_send, att_recv, spread_send,
     spread_recv, part_send, part_recv, og_send, og_recv, sum_send, sum_recv,
 ):
     d = lax.axis_index("dp")
@@ -101,7 +100,8 @@
     rows, _ = upstream.shape
     high, features = projection.shape
     wide = features // chunks
-    half = high // HALVES
+    half = high // 2
+    g = lax.axis_index("groups")
     scaling = HD ** (-0.5)
     pending = []
 
@@ -122,7 +122,10 @@
             barrier, inc=1, device_id={"dp": d, "tensor": lax.rem(t + k, line)},
             device_id_type=MESH,
         )
-    pl.semaphore_wait(barrier, seqs + line - 2)
+    pl.semaphore_signal(
+        barrier, inc=1, device_id={"groups": 1 - g, "dp": d, "tensor": t}, device_id_type=MESH
+    )
+    pl.semaphore_wait(barrier, seqs + line - 1)
 
     others = [lax.rem(d + k, seqs) for k in range(1, seqs)]
     peers = [lax.rem(t + k, line) for k in range(1, line)]
@@ -153,9 +156,9 @@
     def block(j, p):
         return proj_all.at[pl.ds(pl.multiple_of(j * high + p * half, half), half)]
 
-    def proj_send(j, p, source, where, toward):
+    def proj_send(j, source, where, toward):
         sems = right_send if toward is right else left_send
-        one = copy(source, block(j, p), sems.at[j, p], proj_recv.at[j, p], d, toward)
+        one = copy(source, block(j, g), sems.at[j], proj_recv.at[j], d, toward)
 
         @pl.when(where)
         def _():
@@ -163,31 +166,43 @@
 
         pending.append((where, one))
 
-    def proj_own(p):
-        source = projection.at[pl.ds(p * half, half)]
-        proj_send(t, p, source, t < line - 1, right)
-        proj_send(t, p, source, t > 0, left)
+    def proj_own():
+        source = projection.at[pl.ds(pl.multiple_of(g * half, half), half)]
+        proj_send(t, source, t < line - 1, right)
+        proj_send(t, source, t > 0, left)
+
+    def swap(j, p):
+        return pltpu.make_async_remote_copy(
+            src_ref=block(j, p), dst_ref=block(j, p), send_sem=swap_send.at[j],
+            recv_sem=swap_recv.at[j], device_id={"groups": 1 - g, "dp": d, "tensor": t},
+            device_id_type=MESH,
+        )
 
     def proj_step(k):
-        for p in range(HALVES):
-            from_left, from_right = jnp.maximum(t - k, 0), jnp.minimum(t + k, line - 1)
-            for j, here, toward, on in (
-                (from_left, t >= k, right, t < line - 1),
-                (from_right, t + k < line, left, t > 0),
-            ):
-                dst = block(j, p)
-
-                @pl.when(here)
-                def _(dst=dst, j=j):
-                    copy(dst, dst, right_send.at[j, p], proj_recv.at[j, p], d, right).wait_recv()
-
-                if k < line - 1:
-                    proj_send(j, p, dst, jnp.logical_and(here, on), toward)
-
-    early = max(1, chunks // 2)
+        from_left, from_right = jnp.maximum(t - k, 0), jnp.minimum(t + k, line - 1)
+        for j, here, toward, on in (
+            (from_left, t >= k, right, t < line - 1),
+            (from_right, t + k < line, left, t > 0),
+        ):
+            dst = block(j, g)
+            across = swap(j, g)
+
+            @pl.when(here)
+            def _(dst=dst, j=j, across=across):
+                copy(dst, dst, right_send.at[j], proj_recv.at[j], d, right).wait_recv()
+                across.start()
+
+            pending.append((here, across))
+            if k < line - 1:
+                proj_send(j, dst, jnp.logical_and(here, on), toward)
+
+    def wait_swaps():
+        for j in peers:
+            swap(j, 1 - g).wait_recv()
+
+    early = max(1, chunks // 4)
     for c in range(early):
         send_upstream(c)
-    proj_own(0)
 
     ends = []
     sofar = lengths[0, 0]
@@ -215,8 +230,7 @@
         )
         one.start()
         pending.append((None, one))
-    for p in range(1, HALVES):
-        proj_own(p)
+    proj_own()
     for c in range(chunks):
         up_all[c, mine] = upstream[:, pl.ds(pl.multiple_of(d * features + c * wide, wide), wide)]
     proj_all[pl.ds(pl.multiple_of(t * high, high), high), :] = projection[...]
@@ -267,9 +281,12 @@
 
                 pending.append((go, one))
 
+    def own_term(c):
+        cols = slice(c * wide, (c + 1) * wide)
+        grad_projection[:, cols] = dot(att_all[t], up_all[c], 0, 0)
+
     def own_chunk(c):
         cols = slice(c * wide, (c + 1) * wide)
-        grad_projection[:, cols] = dot(att_all[t], up_all[c], 0, 0)
         for way, there in ((0, t > 0), (1, t < line - 1)):
             dst = landed.at[way, t, c]
 
@@ -280,9 +297,11 @@
                 ).wait_recv()
                 grad_projection[:, cols] += landed[way, t, c].astype(F32)
 
+    def part_copy(o):
+        return copy(part.at[o], part_in.at[d], part_send.at[o], part_recv.at[d], o, t)
+
     def out_partials():
-        for c in range(chunks):
-            wait_upstream(c)
+        wait_swaps()
         for o in others + [d]:
             at = pl.ds(pl.multiple_of(o * rows, rows), rows)
             piece = dot(up_all[0, at], proj_all[:, :wide], 1, 1)
@@ -292,12 +311,11 @@
                 part_in[d] = piece.astype(BF16)
                 continue
             part[o] = piece.astype(BF16)
-            one = copy(part.at[o], part_in.at[d], part_send.at[o], part_recv.at[d], o, t)
-            one.start()
-            pending.append((None, one))
+            part_copy(o).start()
 
     def out_sum():
         for o in others:
+            pending.append((None, part_copy(o)))
             dst = part_in.at[o]
             copy(dst, dst, part_send.at[o], part_recv.at[o], o, t).wait_recv()
         whole = sum(part_in[n].astype(F32) for n in range(seqs)).astype(BF16)
@@ -309,15 +327,28 @@
             one.start()
             pending.append((None, one))
 
+    inner = jnp.logical_and(t > 0, t < line - 1)
     for c in range(chunks):
+        if c == chunks // 2:
+            for later in range(c, chunks):
+                wait_upstream(later)
+
+            @pl.when(inner)
+            def _():
+                out_partials()
+
+        if c == chunks - 1:
+
+            @pl.when(jnp.logical_not(inner))
+            def _():
+                out_partials()
+
+            out_sum()
         sum_chunk(c)
-        if c == 0:
-            for k in range(2, line):
-                proj_step(k)
-        if c == max(0, chunks - 3):
-            out_partials()
-        if c == max(0, chunks - 2):
-            out_sum()
+        if c < line - 2:
+            proj_step(c + 2)
+    for c in range(chunks):
+        own_term(c)
 
     for o in peers:
         dst = og_in.at[o]
@@ -349,6 +380,40 @@
                 one.wait_send()
 
 
+def hand_on(pieces, *refs):
+    count = (len(refs) - 2) // 3
+    ins, outs, held = refs[:count], refs[count:2 * count], refs[2 * count:3 * count]
+    in_sems, out_sems = refs[3 * count:]
+    steps = []
+    for n, (i, o, h) in enumerate(zip(ins, outs, held)):
+        size = i.shape[0] // pieces
+        for p in range(pieces):
+            at = pl.ds(p * size, size)
+            steps.append((
+                pltpu.make_async_copy(i.at[at], h.at[at], in_sems.at[n, p]),
+                pltpu.make_async_copy(h.at[at], o.at[at], out_sems.at[n, p]),
+            ))
+    for take, _ in steps:
+        take.start()
+    for take, give in steps:
+        take.wait()
+        give.start()
+    for _, give in steps:
+        give.wait()
+
+
+def handed_on(arrays, pieces=2):
+    held = pl.BlockSpec(memory_space=pl.ANY)
+    return pl.pallas_call(
+        functools.partial(hand_on, pieces),
+        out_shape=tuple(jax.ShapeDtypeStruct(a.shape, a.dtype) for a in arrays),
+        in_specs=[held] * len(arrays),
+        out_specs=(held,) * len(arrays),
+        scratch_shapes=[pltpu.VMEM(a.shape, a.dtype) for a in arrays]
+        + [pltpu.SemaphoreType.DMA((len(arrays), pieces))] * 2,
+    )(*arrays)
+
+
 def fused_shards(seqs, line, query, keys, values, upstream, projection, lengths):
     total, width = query.shape
     rows = upstream.shape[0]
@@ -358,7 +423,7 @@
     dma = pltpu.SemaphoreType.DMA
     vmem = pltpu.VMEM
     whole = pl.BlockSpec(memory_space=pltpu.VMEM)
-    return pl.pallas_call(
+    grads = pl.pallas_call(
         functools.partial(kernel, seqs, line, chunks),
         out_shape=(
             jax.ShapeDtypeStruct(query.shape, BF16),
@@ -381,7 +446,7 @@
             vmem((2, line, chunks, high, wide), BF16),
             vmem((2, line, chunks, high, wide), BF16),
             dma((seqs, chunks)), dma((seqs, chunks)),
-            dma((line, HALVES)), dma((line, HALVES)), dma((line, HALVES)),
+            dma((line,)), dma((line,)), dma((line,)), dma((line,)), dma((line,)),
             dma((line,)), dma((line,)),
             dma((seqs,)), dma((seqs,)),
             dma((seqs,)), dma((seqs,)),
@@ -390,6 +455,7 @@
         ],
         compiler_params=pltpu.CompilerParams(collective_id=0, has_side_effects=True),
     )(query, keys, values, upstream, projection, lengths)
+    return handed_on(grads)
 
 
 def solution(mesh):
@@ -403,7 +469,9 @@
             and 1 < line
             and max(seqs, line) <= MOST_STEPS
             and projection.shape[1] % (CHUNKS * LANES) == 0
-            and upstream.shape[0] % (2 * HALVES * 8) == 0
+            and upstream.shape[0] % 32 == 0
+            and mesh.shape["groups"] == 2
+            and line - 2 <= CHUNKS // 2
             and upstream.shape[0] * line == query.shape[0]
         )
         if fits:

time: 95.1 us -> 70.3 us (0.74); the launches traced: 93.2 us -> 69.8 us
  Pallas kernels: 85.6 us -> 69.2 us
  local copies, waits for them, and re-layouts: 7 us -> 0 us
    pallas_call x1, Pallas kernels: 85.6 us -> 66.8 us  [fused_shards(): pl.pallas_call(functools.partial(kernel, seqs, line, chunks), out_shape=(...]
    unnamed x4 -> x0, local copies, waits for them, and re-layouts: 7 us -> none
    pallas_call x0 -> x1, Pallas kernels: none -> 2.36 us  [handed_on(): pl.pallas_call(functools.partial(hand_on, pieces), out_shape=tuple((jax.S...]
where the time goes in v2:
time: 70.3 us; the launch traced here: 69.8 us
  Pallas kernels  69.2 us (98%)
    pallas_call x1, Pallas kernels, fused_shards(): pl.pallas_call(functools.partial(kernel, seqs, line, chunks), out_shape=(...  66.8 us
    pallas_call x1, Pallas kernels, handed_on(): pl.pallas_call(functools.partial(hand_on, pieces), out_shape=tuple((jax.S...  2.36 us

profile of v2, /device:TPU:1, one launch (start us, length us, event | category | flops | bytes accessed | tf_op | source)
XLA Modules:
  0.0 69.8 jit_solution(3882669920364734997)
XLA Ops:
  0.6 66.8 %shard_map.93 = (bf16[512,128]{1,0:T(8,128)(2,1)}, bf16[512,128]{1,0:T(8,128)(2,1)}, bf16[512,128]{1,0:T(8,128)(2,1)}, f32[128,2048]{1,0:T(8,128)}) custom-call(bf16[512,128]{1,0:T(8,128)(2,1)} %query.1, bf16[512,128]{1,0:T(8,128)(2,1)} %keys.1, bf16[512,128]{1,0:T(8,128)(2,1)} %values.1, bf16[128,8192]{1,0:T(8,128)(2,1)} %upstream.1, ...), custom_call_target="tpu_custom_call" | custom-call | tf_op jit(solution)/shard_map/pallas_call | solution.py:426
  67.4 2.4 %shard_map.94 = (bf16[512,128]{1,0:T(8,128)(2,1)}, bf16[512,128]{1,0:T(8,128)(2,1)}, bf16[512,128]{1,0:T(8,128)(2,1)}, f32[128,2048]{1,0:T(8,128)}) custom-call(bf16[512,128]{1,0:T(8,128)(2,1)} %get-tuple-element.8.refs_0_, bf16[512,128]{1,0:T(8,128)(2,1)} %get-tuple-element.9.refs_1_, bf16[512,128]{1,0:T(8,128)(2,1)} %get-tuple-element.10.refs_2_, ...), custom_call_target="tpu_custom_call" | custom-call | tf_op jit(solution)/shard_map/pallas_call | solution.py:407

commit v3 on v2

--- a/solution.py
+++ b/solution.py
@@ -90,7 +90,7 @@
     seqs, line, chunks,
     query, keys, values, upstream, projection, lengths,
     grad_query, grad_keys, grad_values, grad_projection,
-    probs_ref, att_own, att_all, up_all, proj_all, part, part_in, og_own, og_in, stage, landed,
+    probs_ref, att_own, att_all, att_turned, out_acc, up_all, proj_all, part, part_in, og_own, og_in, stage, landed,
     up_send, up_recv, right_send, left_send, proj_recv, swap_send, swap_recv, att_send, att_recv, spread_send,
     spread_recv, part_send, part_recv, og_send, og_recv, sum_send, sum_recv,
 ):
@@ -143,12 +143,7 @@
             one.start()
             pending.append((None, one))
 
-    waited = set()
-
     def wait_upstream(c):
-        if c in waited:
-            return
-        waited.add(c)
         for o in others:
             dst = up_all.at[c, pl.ds(pl.multiple_of(o * rows, rows), rows)]
             copy(dst, dst, up_send.at[o, c], up_recv.at[o, c], o, t).wait_recv()
@@ -156,15 +151,17 @@
     def block(j, p):
         return proj_all.at[pl.ds(pl.multiple_of(j * high + p * half, half), half)]
 
-    def proj_send(j, source, where, toward):
+    def proj_send(j, source, where, toward, run=True, keep=True):
         sems = right_send if toward is right else left_send
         one = copy(source, block(j, g), sems.at[j], proj_recv.at[j], d, toward)
-
-        @pl.when(where)
-        def _():
-            one.start()
-
-        pending.append((where, one))
+        if run:
+
+            @pl.when(where)
+            def _():
+                one.start()
+
+        if keep:
+            pending.append((where, one))
 
     def proj_own():
         source = projection.at[pl.ds(pl.multiple_of(g * half, half), half)]
@@ -178,7 +175,7 @@
             device_id_type=MESH,
         )
 
-    def proj_step(k):
+    def proj_step(k, run=True):
         from_left, from_right = jnp.maximum(t - k, 0), jnp.minimum(t + k, line - 1)
         for j, here, toward, on in (
             (from_left, t >= k, right, t < line - 1),
@@ -186,15 +183,17 @@
         ):
             dst = block(j, g)
             across = swap(j, g)
-
-            @pl.when(here)
-            def _(dst=dst, j=j, across=across):
-                copy(dst, dst, right_send.at[j], proj_recv.at[j], d, right).wait_recv()
-                across.start()
-
-            pending.append((here, across))
+            if not run:
+                pending.append((here, across))
+            else:
+
+                @pl.when(here)
+                def _(dst=dst, j=j, across=across):
+                    copy(dst, dst, right_send.at[j], proj_recv.at[j], d, right).wait_recv()
+                    across.start()
+
             if k < line - 1:
-                proj_send(j, dst, jnp.logical_and(here, on), toward)
+                proj_send(j, dst, jnp.logical_and(here, on), toward, run, not run)
 
     def wait_swaps():
         for j in peers:
@@ -203,6 +202,7 @@
     early = max(1, chunks // 4)
     for c in range(early):
         send_upstream(c)
+    proj_own()
 
     ends = []
     sofar = lengths[0, 0]
@@ -230,7 +230,6 @@
         )
         one.start()
         pending.append((None, one))
-    proj_own()
     for c in range(chunks):
         up_all[c, mine] = upstream[:, pl.ds(pl.multiple_of(d * features + c * wide, wide), wide)]
     proj_all[pl.ds(pl.multiple_of(t * high, high), high), :] = projection[...]
@@ -250,8 +249,7 @@
         dst = att_all.at[:, pl.ds(pl.multiple_of(o * rows, rows), rows)]
         copy(dst, dst, spread_send.at[o], spread_recv.at[o], o, t).wait_recv()
 
-    def sum_chunk(c):
-        wait_upstream(c)
+    def sum_chunk(c, run=True):
         for k in range(line - 1, 0, -1):
             for way, head, go, first, toward in (
                 (0, jnp.minimum(t + k, line - 1), t + k < line, t == 0, right),
@@ -262,9 +260,15 @@
                     sum_send.at[way, head, c], sum_recv.at[way, head, c], d, toward,
                 )
 
+                if not run:
+                    pending.append((go, one))
+                    continue
+
                 @pl.when(go)
                 def _(way=way, head=head, first=first, one=one):
-                    term = dot(att_all[head], up_all[c], 0, 0)
+                    if c == 0:
+                        att_turned[head] = att_all[head].T
+                    term = dot(att_turned[head], up_all[c], 1, 0)
 
                     @pl.when(first)
                     def _():
@@ -279,11 +283,12 @@
 
                     one.start()
 
-                pending.append((go, one))
 
     def own_term(c):
         cols = slice(c * wide, (c + 1) * wide)
-        grad_projection[:, cols] = dot(att_all[t], up_all[c], 0, 0)
+        if c == 0:
+            att_turned[t] = att_all[t].T
+        grad_projection[:, cols] = dot(att_turned[t], up_all[c], 1, 0)
 
     def own_chunk(c):
         cols = slice(c * wide, (c + 1) * wide)
@@ -300,17 +305,20 @@
     def part_copy(o):
         return copy(part.at[o], part_in.at[d], part_send.at[o], part_recv.at[d], o, t)
 
+    def out_term(c):
+        piece = dot(up_all[c], proj_all[:, c * wide:(c + 1) * wide], 1, 1)
+        if c == 0:
+            out_acc[...] = piece
+        else:
+            out_acc[...] += piece
+
     def out_partials():
-        wait_swaps()
         for o in others + [d]:
             at = pl.ds(pl.multiple_of(o * rows, rows), rows)
-            piece = dot(up_all[0, at], proj_all[:, :wide], 1, 1)
-            for c in range(1, chunks):
-                piece += dot(up_all[c, at], proj_all[:, c * wide:(c + 1) * wide], 1, 1)
             if o is d:
-                part_in[d] = piece.astype(BF16)
+                part_in[d] = out_acc[at, :].astype(BF16)
                 continue
-            part[o] = piece.astype(BF16)
+            part[o] = out_acc[at, :].astype(BF16)
             part_copy(o).start()
 
     def out_sum():
@@ -328,27 +336,49 @@
             pending.append((None, one))
 
     inner = jnp.logical_and(t > 0, t < line - 1)
-    for c in range(chunks):
-        if c == chunks // 2:
-            for later in range(c, chunks):
-                wait_upstream(later)
-
-            @pl.when(inner)
-            def _():
-                out_partials()
-
-        if c == chunks - 1:
-
-            @pl.when(jnp.logical_not(inner))
-            def _():
-                out_partials()
-
-            out_sum()
-        sum_chunk(c)
-        if c < line - 2:
-            proj_step(c + 2)
-    for c in range(chunks):
+    outer = jnp.logical_not(inner)
+    wait_upstream(0)
+    for k in range(2, line - 1):
+
+        @pl.when(inner)
+        def _(k=k):
+            proj_step(k)
+
+    sum_chunk(0)
+    for k in range(2, line - 1):
+
+        @pl.when(outer)
+        def _(k=k):
+            proj_step(k)
+
+    wait_upstream(1)
+    sum_chunk(1)
+    proj_step(line - 1)
+    wait_swaps()
+    out_term(0)
+    out_term(1)
+    for c in range(2, chunks - 1):
+        wait_upstream(c)
+        out_term(c)
+
+        @pl.when(outer)
+        def _(c=c):
+            sum_chunk(c)
+
+    wait_upstream(chunks - 1)
+    out_term(chunks - 1)
+    out_partials()
+    for c in range(2, chunks - 1):
+
+        @pl.when(inner)
+        def _(c=c):
+            sum_chunk(c)
+
+    for c in range(chunks - 1):
         own_term(c)
+    out_sum()
+    sum_chunk(chunks - 1)
+    own_term(chunks - 1)
 
     for o in peers:
         dst = og_in.at[o]
@@ -370,6 +400,10 @@
     for c in range(chunks):
         own_chunk(c)
 
+    for k in range(1, line):
+        proj_step(k, False)
+    for c in range(chunks):
+        sum_chunk(c, False)
     for where, one in pending:
         if where is None:
             one.wait_send()
@@ -437,6 +471,8 @@
             vmem((total, total), F32),
             vmem((line, rows, width), BF16),
             vmem((line, seqs * rows, width), BF16),
+            vmem((line, width, seqs * rows), BF16),
+            vmem((seqs * rows, line * high), F32),
             vmem((chunks, seqs * rows, wide), BF16),
             vmem((line * high, features), BF16),
             vmem((seqs, rows, line * high), BF16),
@@ -471,7 +507,7 @@
             and projection.shape[1] % (CHUNKS * LANES) == 0
             and upstream.shape[0] % 32 == 0
             and mesh.shape["groups"] == 2
-            and line - 2 <= CHUNKS // 2
+            and 3 <= line
             and upstream.shape[0] * line == query.shape[0]
         )
         if fits:

time: 70.3 us -> 69.9 us (level)
  no operation moved by 1% of the time
where the time goes in v3:
time: 69.9 us; the launch traced here: 69.7 us
  Pallas kernels  69 us (99%)
    pallas_call x1, Pallas kernels, fused_shards(): pl.pallas_call(functools.partial(kernel, seqs, line, chunks), out_shape=(...  66.7 us
    pallas_call x1, Pallas kernels, handed_on(): pl.pallas_call(functools.partial(hand_on, pieces), out_shape=tuple((jax.S...  2.36 us

profile of v3, /device:TPU:1, one launch (start us, length us, event | category | flops | bytes accessed | tf_op | source)
XLA Modules:
  0.0 69.7 jit_solution(3898812634751805623)
XLA Ops:
  0.6 66.7 %shard_map.93 = (bf16[512,128]{1,0:T(8,128)(2,1)}, bf16[512,128]{1,0:T(8,128)(2,1)}, bf16[512,128]{1,0:T(8,128)(2,1)}, f32[128,2048]{1,0:T(8,128)}) custom-call(bf16[512,128]{1,0:T(8,128)(2,1)} %query.1, bf16[512,128]{1,0:T(8,128)(2,1)} %keys.1, bf16[512,128]{1,0:T(8,128)(2,1)} %values.1, bf16[128,8192]{1,0:T(8,128)(2,1)} %upstream.1, ...), custom_call_target="tpu_custom_call" | custom-call | tf_op jit(solution)/shard_map/pallas_call | solution.py:460
  67.3 2.4 %shard_map.94 = (bf16[512,128]{1,0:T(8,128)(2,1)}, bf16[512,128]{1,0:T(8,128)(2,1)}, bf16[512,128]{1,0:T(8,128)(2,1)}, f32[128,2048]{1,0:T(8,128)}) custom-call(bf16[512,128]{1,0:T(8,128)(2,1)} %get-tuple-element.8.refs_0_, bf16[512,128]{1,0:T(8,128)(2,1)} %get-tuple-element.9.refs_1_, bf16[512,128]{1,0:T(8,128)(2,1)} %get-tuple-element.10.refs_2_, ...), custom_call_target="tpu_custom_call" | custom-call | tf_op jit(solution)/shard_map/pallas_call | solution.py:441

commit v4 on v3

--- a/solution.py
+++ b/solution.py
@@ -321,9 +321,11 @@
             part[o] = out_acc[at, :].astype(BF16)
             part_copy(o).start()
 
+    def og_copy(o):
+        return copy(og_own.at[o], og_in.at[t], og_send.at[o], og_recv.at[t], d, o)
+
     def out_sum():
         for o in others:
-            pending.append((None, part_copy(o)))
             dst = part_in.at[o]
             copy(dst, dst, part_send.at[o], part_recv.at[o], o, t).wait_recv()
         whole = sum(part_in[n].astype(F32) for n in range(seqs)).astype(BF16)
@@ -331,9 +333,7 @@
             og_own[q] = whole[:, q * HD:(q + 1) * HD]
         og_in[t] = og_own[t]
         for o in peers:
-            one = copy(og_own.at[o], og_in.at[t], og_send.at[o], og_recv.at[t], d, o)
-            one.start()
-            pending.append((None, one))
+            og_copy(o).start()
 
     inner = jnp.logical_and(t > 0, t < line - 1)
     outer = jnp.logical_not(inner)
@@ -351,34 +351,36 @@
         def _(k=k):
             proj_step(k)
 
-    wait_upstream(1)
-    sum_chunk(1)
-    proj_step(line - 1)
-    wait_swaps()
-    out_term(0)
-    out_term(1)
-    for c in range(2, chunks - 1):
-        wait_upstream(c)
-        out_term(c)
-
-        @pl.when(outer)
-        def _(c=c):
+    @pl.when(outer)
+    def _():
+        for c in range(1, chunks):
+            wait_upstream(c)
             sum_chunk(c)
-
-    wait_upstream(chunks - 1)
-    out_term(chunks - 1)
-    out_partials()
-    for c in range(2, chunks - 1):
-
-        @pl.when(inner)
-        def _(c=c):
+            if c == 1:
+                proj_step(line - 1)
+        wait_swaps()
+        for c in range(chunks):
+            out_term(c)
+        out_partials()
+        for c in range(chunks):
+            own_term(c)
+        out_sum()
+
+    @pl.when(inner)
+    def _():
+        proj_step(line - 1)
+        wait_swaps()
+        for c in range(chunks):
+            if c > 0:
+                wait_upstream(c)
+            out_term(c)
+        out_partials()
+        for c in range(1, chunks):
             sum_chunk(c)
-
-    for c in range(chunks - 1):
-        own_term(c)
-    out_sum()
-    sum_chunk(chunks - 1)
-    own_term(chunks - 1)
+            if c == 1:
+                out_sum()
+        for c in range(chunks):
+            own_term(c)
 
     for o in peers:
         dst = og_in.at[o]
@@ -400,6 +402,10 @@
     for c in range(chunks):
         own_chunk(c)
 
+    for o in others:
+        pending.append((None, part_copy(o)))
+    for o in peers:
+        pending.append((None, og_copy(o)))
     for k in range(1, line):
         proj_step(k, False)
     for c in range(chunks):

time: 69.9 us -> 69.5 us (level)
  no operation moved by 1% of the time
where the time goes in v4:
time: 69.5 us; the launch traced here: 69.3 us
  Pallas kernels  68.7 us (99%)
    pallas_call x1, Pallas kernels, fused_shards(): pl.pallas_call(functools.partial(kernel, seqs, line, chunks), out_shape=(...  66.3 us
    pallas_call x1, Pallas kernels, handed_on(): pl.pallas_call(functools.partial(hand_on, pieces), out_shape=tuple((jax.S...  2.36 us

profile of v4, /device:TPU:1, one launch (start us, length us, event | category | flops | bytes accessed | tf_op | source)
XLA Modules:
  0.0 69.3 jit_solution(2021909489004365718)
XLA Ops:
  0.6 66.3 %shard_map.93 = (bf16[512,128]{1,0:T(8,128)(2,1)}, bf16[512,128]{1,0:T(8,128)(2,1)}, bf16[512,128]{1,0:T(8,128)(2,1)}, f32[128,2048]{1,0:T(8,128)}) custom-call(bf16[512,128]{1,0:T(8,128)(2,1)} %query.1, bf16[512,128]{1,0:T(8,128)(2,1)} %keys.1, bf16[512,128]{1,0:T(8,128)(2,1)} %values.1, bf16[128,8192]{1,0:T(8,128)(2,1)} %upstream.1, ...), custom_call_target="tpu_custom_call" | custom-call | tf_op jit(solution)/shard_map/pallas_call | solution.py:466
  67.0 2.4 %shard_map.94 = (bf16[512,128]{1,0:T(8,128)(2,1)}, bf16[512,128]{1,0:T(8,128)(2,1)}, bf16[512,128]{1,0:T(8,128)(2,1)}, f32[128,2048]{1,0:T(8,128)}) custom-call(bf16[512,128]{1,0:T(8,128)(2,1)} %get-tuple-element.8.refs_0_, bf16[512,128]{1,0:T(8,128)(2,1)} %get-tuple-element.9.refs_1_, bf16[512,128]{1,0:T(8,128)(2,1)} %get-tuple-element.10.refs_2_, ...), custom_call_target="tpu_custom_call" | custom-call | tf_op jit(solution)/shard_map/pallas_call | solution.py:447
